TPU v7x, 32 devices: a whole 2x2x4 slice. The times are simulated.
32 devices in a mesh: fsdp: 16 (over z, y, core), grp: 2 (over x).
Axes of the slice: x: 2, y: 2, z: 4, core: 2. Of those that a mesh axis runs over, the one named last changes fastest.
Arguments:
- hidden: bfloat16 [8192, 3072], P('fsdp', 'grp'), may hold values from -16 to 16
- queries: bfloat16 [8192, 1536], P('fsdp', 'grp'), may hold values from -6 to 6
- attn_keys: bfloat16 [8192, 1536], P('fsdp', 'grp'), may hold values from -6 to 6
- w_value: bfloat16 [1536, 3072], P('fsdp', 'grp'), may hold values from -1 to 1
- w_out: bfloat16 [1536, 3072], P('fsdp', 'grp'), may hold values from -1 to 1
- alpha: float32 [3072], P('grp'), may hold values from 0.05 to 0.5
- out_grad: bfloat16 [8192, 3072], P('fsdp', 'grp'), may hold values from -6 to 6
Outputs:
- new_hidden: bfloat16 [8192, 3072], P('fsdp', 'grp')
- grad_hidden: bfloat16 [8192, 3072], P('fsdp', 'grp')
- grad_queries: bfloat16 [8192, 1536], P('fsdp', 'grp')
- grad_keys: bfloat16 [8192, 1536], P('fsdp', 'grp')
- grad_w_value: float32 [1536, 3072], P('fsdp', 'grp')
- grad_w_out: float32 [1536, 3072], P('fsdp', 'grp')
All inputs are finite; a program needn't handle non-finite values.
Results may differ from a plain program's by a relative error of at most 0.012.
The roundings to bfloat16 on the way count: a program that leaves them out, or rounds other values in their place, can miss the bound.
Values may be sent and summed in bfloat16 or wider, within the bound.
A program may use at most 192 MiB of HBM per device.

v0:
```python
import jax
import jax.numpy as jnp
from jax import lax
from jax.sharding import PartitionSpec as P

D = 3072
HS = 128
EPS = 1e-06


def contract_last(left, right):
    return lax.dot_general(
        left, right, (((1,), (1,)), ((), ())), preferred_element_type=jnp.float32
    )


def contract_first(left, right):
    return lax.dot_general(
        left, right, (((0,), (0,)), ((), ())), preferred_element_type=jnp.float32
    )


def causal_probs(query_head, key_head):
    length = query_head.shape[0]
    score_scale = query_head.shape[1] ** (-0.5)
    scores = contract_last(query_head, key_head) * score_scale
    row_pos = lax.broadcasted_iota(jnp.int32, (length, length), 0)
    col_pos = lax.broadcasted_iota(jnp.int32, (length, length), 1)
    scores = jnp.where(row_pos >= col_pos, scores, -1e30)
    row_peak = jnp.max(scores, axis=1, keepdims=True)
    exp_terms = jnp.exp(scores - row_peak)
    return exp_terms / jnp.sum(exp_terms, axis=1, keepdims=True)


def head_forward(items):
    query_head, key_head, value_head = items
    attn_prob = causal_probs(query_head, key_head)
    return jnp.dot(
        attn_prob.astype(jnp.bfloat16), value_head, preferred_element_type=jnp.float32
    ).astype(jnp.bfloat16)


def head_backward(items):
    query_head, key_head, value_head, grad_head = items
    score_scale = query_head.shape[1] ** (-0.5)
    attn_prob = causal_probs(query_head, key_head)
    prob_half = attn_prob.astype(jnp.bfloat16)
    grad_prob = contract_last(grad_head, value_head)
    row_delta = jnp.sum(attn_prob * grad_prob, axis=1, keepdims=True)
    grad_score = (attn_prob * (grad_prob - row_delta)).astype(jnp.bfloat16)
    grad_query = (
        jnp.dot(grad_score, key_head, preferred_element_type=jnp.float32) * score_scale
    ).astype(jnp.bfloat16)
    grad_key = (contract_first(grad_score, query_head) * score_scale).astype(jnp.bfloat16)
    grad_value = contract_first(prob_half, grad_head).astype(jnp.bfloat16)
    return (grad_query, grad_key, grad_value)


def split_heads(block):
    return block.reshape(block.shape[0], -1, HS).transpose(1, 0, 2)


def join_heads(stacked):
    return stacked.transpose(1, 0, 2).reshape(stacked.shape[1], -1)


def shards(hidden, queries, attn_keys, w_value, w_out, alpha, out_grad):
    half_width = hidden.shape[1]
    value_rows = w_value.astype(jnp.float32)
    out_rows = w_out.astype(jnp.float32)
    row_sums = lax.psum(
        (jnp.sum(value_rows * value_rows, axis=1), jnp.sum(out_rows * out_rows, axis=1)), "grp"
    )
    norm_v = jnp.sqrt(row_sums[0] + EPS)[:, None]
    norm_o = jnp.sqrt(row_sums[1] + EPS)[:, None]
    unit_v = value_rows / norm_v
    unit_o = out_rows / norm_o
    weight_v, weight_o = (
        lax.all_gather(unit_v.astype(jnp.bfloat16), "fsdp", axis=0, tiled=True),
        lax.all_gather(unit_o.astype(jnp.bfloat16), "fsdp", axis=0, tiled=True),
    )
    value_parts = contract_last(hidden, weight_v)
    values_mine = lax.psum_scatter(value_parts, "grp", scatter_dimension=1, tiled=True).astype(
        jnp.bfloat16
    )
    q_heads = split_heads(queries)
    k_heads = split_heads(attn_keys)
    v_heads = split_heads(values_mine)
    attn_mine = join_heads(lax.map(head_forward, (q_heads, k_heads, v_heads)))
    attn_all = lax.all_gather(attn_mine, "grp", axis=1, tiled=True)
    proj = jnp.dot(attn_all, weight_o, preferred_element_type=jnp.float32)
    hidden_f = hidden.astype(jnp.float32)
    keep_rate = 1.0 - alpha
    moments = lax.psum(
        (
            jnp.sum(proj * proj, axis=1),
            jnp.sum(keep_rate * keep_rate * hidden_f * hidden_f, axis=1),
            jnp.sum(keep_rate * alpha * hidden_f * proj, axis=1),
            jnp.sum(alpha * alpha * proj * proj, axis=1),
        ),
        "grp",
    )
    proj_rs = lax.rsqrt(moments[0] / D + EPS)[:, None]
    cross_sum = moments[2][:, None]
    alpha_sum = moments[3][:, None]
    mix_mean = (moments[1][:, None] + 2.0 * proj_rs * cross_sum + proj_rs * proj_rs * alpha_sum) / D
    mix_rs = lax.rsqrt(mix_mean + EPS)
    mixed = hidden_f + alpha * (proj * proj_rs - hidden_f)
    new_hidden = (mixed * mix_rs).astype(jnp.bfloat16)
    grad_out = out_grad.astype(jnp.float32)
    grad_sums = lax.psum(
        (
            jnp.sum(grad_out * keep_rate * hidden_f, axis=1),
            jnp.sum(grad_out * alpha * proj, axis=1),
        ),
        "grp",
    )
    grad_mean = (grad_sums[0][:, None] + proj_rs * grad_sums[1][:, None]) / D
    grad_mix = mix_rs * (grad_out - mixed * mix_rs * mix_rs * grad_mean)
    grad_pn = grad_mix * alpha
    proj_mean = (
        mix_rs * grad_sums[1][:, None]
        - mix_rs * mix_rs * mix_rs * grad_mean * (cross_sum + proj_rs * alpha_sum)
    ) / D
    grad_res = grad_mix * keep_rate
    grad_proj = proj_rs * (grad_pn - proj * proj_rs * proj_rs * proj_mean)
    grad_proj_b = grad_proj.astype(jnp.bfloat16)
    grad_attn_parts = contract_last(grad_proj_b, weight_o)
    grad_attn = lax.psum_scatter(grad_attn_parts, "grp", scatter_dimension=1, tiled=True).astype(
        jnp.bfloat16
    )
    grad_q, grad_k, grad_v = lax.map(
        head_backward, (q_heads, k_heads, v_heads, split_heads(grad_attn))
    )
    grad_values = lax.all_gather(join_heads(grad_v), "grp", axis=1, tiled=True)
    grad_hidden = (
        grad_res + jnp.dot(grad_values, weight_v, preferred_element_type=jnp.float32)
    ).astype(jnp.bfloat16)
    owned = lax.psum_scatter(
        jnp.concatenate(
            (contract_first(grad_values, hidden), contract_first(attn_all, grad_proj_b)), axis=1
        ),
        "fsdp",
        scatter_dimension=0,
        tiled=True,
    )
    gw_v_own = owned[:, :half_width]
    gw_o_own = owned[:, half_width:]
    row_dot = lax.psum(
        (jnp.sum(gw_v_own * unit_v, axis=1), jnp.sum(gw_o_own * unit_o, axis=1)), "grp"
    )
    grad_w_value = (gw_v_own - unit_v * row_dot[0][:, None]) / norm_v
    grad_w_out = (gw_o_own - unit_o * row_dot[1][:, None]) / norm_o
    return (
        new_hidden,
        grad_hidden,
        join_heads(grad_q),
        join_heads(grad_k),
        grad_w_value,
        grad_w_out,
    )


def solution(mesh):
    placed = (
        P("fsdp", "grp"),
        P("fsdp", "grp"),
        P("fsdp", "grp"),
        P("fsdp", "grp"),
        P("fsdp", "grp"),
        P("grp"),
        P("fsdp", "grp"),
    )
    return jax.shard_map(
        shards,
        mesh=mesh,
        in_specs=placed,
        out_specs=(
            P("fsdp", "grp"),
            P("fsdp", "grp"),
            P("fsdp", "grp"),
            P("fsdp", "grp"),
            P("fsdp", "grp"),
            P("fsdp", "grp"),
        ),
        check_vma=False,
    )
```

profile of v0, /device:TPU:0, one launch (start us, length us, event | category | flops | bytes accessed | tf_op | source)
XLA Modules:
  0.0 593.8 jit_solution(14473532207321060292)
XLA Ops:
  8.5 5.9 all-reduce.2
  14.4 1.8 fusion.60
  16.2 55.0 %all-gather.5.cloned.1.call-done = bf16[1536,1536]{1,0:T(8,128)(2,1)} async-done(((bf16[96,1536]{1,0:T(8,128)(2,1)}), bf16[1536,1536]{1,0:T(8,128)(2,1)}) %all-gather.5.cloned.1.call-update) | async-done | bytes 4718608 | tf_op jit(solution)/shard_map/all_gather | solution.py:79
  71.3 7.1 %convolution_bitcast_fusion = f32[512,1536]{0,1:T(8,128)} fusion(bf16[1536,1536]{1,0:T(8,128)(2,1)} %all-gather.5.cloned.1.call-done, bf16[512,1536]{1,0:T(8,128)(2,1)} %param.11), kind=kOutput, calls=%fused_computation.68 | convolution fusion | flops 2415919104 | bytes 9437184 | tf_op jit(solution)/shard_map/dot_general | solution.py:12
  81.6 39.0 %reduce-scatter.6.cloned.1.call-done = f32[512,768]{0,1:T(8,128)} async-done(((f32[512,1536]{0,1:T(8,128)}), f32[512,768]{0,1:T(8,128)}) %reduce-scatter.6.cloned.1.call-update) | async-done | bytes 1572880 | tf_op jit(solution)/shard_map/reduce_scatter | solution.py:83
  123.3 11.8 %while.24 = (s32[]{:T(128)}, bf16[6,512,128]{1,2,0:T(8,128)(2,1)S(1)}, bf16[6,512,128]{2,1,0:T(8,128)(2,1)S(1)}, bf16[6,512,128]{2,1,0:T(8,128)(2,1)S(1)}, bf16[6,512,128]{2,1,0:T(8,128)(2,1)}, /*index=5*/s32[]{:T(128)}) while((s32[]{:T(128)}, bf16[6,512,128]{1,2,0:T(8,128)(2,1)S(1)}, bf16[6,512,128]{2,1,0:T(8,128)(2,1)S(1)}, ...), condition=%wide.region_6.7_spmd, body=%wide.region_3.6_spmd.sunk | while | flops 136641536 | bytes 4205653 | solution.py:89
  136.1 40.5 %all-gather.9.cloned.1.call-done = bf16[1536,1536]{1,0:T(8,128)(2,1)} async-done(((bf16[96,1536]{1,0:T(8,128)(2,1)}), bf16[1536,1536]{1,0:T(8,128)(2,1)}) %all-gather.9.cloned.1.call-update) | async-done | bytes 4718608 | tf_op jit(solution)/shard_map/all_gather | solution.py:80
  176.6 27.7 %all-gather.7.cloned.1.call-done = bf16[512,1536]{0,1:T(8,128)(2,1)} async-done(((bf16[512,768]{0,1:T(8,128)(2,1)}), bf16[512,1536]{0,1:T(8,128)(2,1)}) %all-gather.7.cloned.1.call-update) | async-done | bytes 1572880 | tf_op jit(solution)/shard_map/all_gather | solution.py:90
  204.3 8.4 %fusion.43 = (f32[512]{0:T(512)S(1)}, f32[512]{0:T(512)S(1)}, f32[512]{0:T(512)S(1)}, f32[512]{0:T(512)S(1)}, f32[512]{0:T(512)S(1)}, /*index=5*/f32[512]{0:T(512)S(1)}, f32[512,1536]{1,0:T(8,128)S(1)}) fusion(bf16[512,1536]{1,0:T(8,128)(2,1)} %param.17, f32[1536]{0:T(1024)S(1)} %copy-done.14, f32[1536]{0:T(1024)S(1)} %get-tuple-element.182, ...), kind=kOutput, calls=%fused_computation.72 | convolution fusion | flops 2430858240 | bytes 12625920 | tf_op jit(solution)/shard_map/dot_general | solution.py:91
  212.7 6.9 %all-reduce.1 = (f32[512]{0:T(512)S(1)}, f32[512]{0:T(512)S(1)}, f32[512]{0:T(512)S(1)}, f32[512]{0:T(512)S(1)}, f32[512]{0:T(512)S(1)}, /*index=5*/f32[512]{0:T(512)S(1)}) all-reduce(f32[512]{0:T(512)S(1)} %get-tuple-element.126, f32[512]{0:T(512)S(1)} %get-tuple-element.130, ...), channel_id=1, replica_groups=mesh['fsdp'=16,'grp'=2] {'grp'}, use_global_device_ids=true, to_apply=%region_16.17 | all-reduce | flops 3072 | bytes 24576 | tf_op jit(solution)/shard_map/psum | solution.py:94
  219.7 4.5 multiply_convert_fusion.1
  225.4 4.3 fusion.65
  229.7 44.7 %reduce-scatter.8.cloned.1.call-done = f32[512,768]{1,0:T(8,128)} async-done(((f32[512,1536]{1,0:T(8,128)}), f32[512,768]{1,0:T(8,128)}) %reduce-scatter.8.cloned.1.call-update) | async-done | bytes 1572880 | tf_op jit(solution)/shard_map/reduce_scatter | solution.py:129
  278.2 47.0 %while.25 = (s32[]{:T(128)}, bf16[6,512,128]{1,2,0:T(8,128)(2,1)}, bf16[6,512,128]{1,2,0:T(8,128)(2,1)S(1)}, bf16[6,512,128]{1,2,0:T(8,128)(2,1)S(1)}, bf16[6,51...) while((s32[]{:T(128)}, bf16[6,512,128]{1,2,0:T(8,128)(2,1)}, ...), condition=%wide.region_26.27_spmd, body=%wide.region_22.26_spmd.sunk | while | flops 340589056 | bytes 11821177 | solution.py:132
  326.2 8.5 %fusion.67 = f32[1536,1536]{0,1:T(8,128)} fusion(bf16[512,1536]{0,1:T(8,128)(2,1)} %all-gather.7.cloned.1.call-done, bf16[512,1536]{1,0:T(8,128)(2,1)} %copy-done.11), kind=kOutput, calls=%fused_computation.114 | convolution fusion | flops 2415919104 | bytes 12582912 | tf_op jit(solution)/shard_map/dot_general | solution.py:18
  334.7 18.8 %all-gather.11.cloned.1.call-done = bf16[512,1536]{0,1:T(8,128)(2,1)} async-done(((bf16[512,768]{0,1:T(8,128)(2,1)}), bf16[512,1536]{0,1:T(8,128)(2,1)}) %all-gather.11.cloned.1.call-update) | async-done | bytes 1572880 | tf_op jit(solution)/shard_map/all_gather | solution.py:135
  353.5 4.2 fusion.66
  357.8 7.2 %pad_maximum_fusion = f32[1536,3072]{0,1:T(8,128)} fusion(f32[1536,1536]{0,1:T(8,128)S(1)} %copy-done, f32[1536,1536]{0,1:T(8,128)S(1)} %fusion.66), kind=kLoop, calls=%fused_computation.57 | loop fusion | flops 4718592 | bytes 37748736 | tf_op jit(solution)/shard_map/concatenate | solution.py:140
  365.0 18.7 %copy.57 = f32[1536,3072]{1,0:T(8,128)} copy(f32[1536,3072]{0,1:T(8,128)} %pad_maximum_fusion) | data formatting | bytes 37748736
  387.1 9.9 %fusion.51 = bf16[512,1536]{1,0:T(8,128)(2,1)} fusion(bf16[512,1536]{0,1:T(8,128)(2,1)} %all-gather.11.cloned.1.call-done, bf16[1536,1536]{1,0:T(8,128)(2,1)} %all-gather.5.cloned.1.call-done, bf16[512,1536]{1,0:T(8,128)(2,1)S(1)} %copy-done.9, f32[512]{0:T(512)S(1)} %get-tuple-element.187, f32[1536]{0:T(1024)S(1)} %get-tuple-element.185, ...), kind=kOutput, calls=%fused_computation.82 | convolution fusion | flops 2426929152 | bytes 14174208 | tf_op jit(solution)/shard_map/dot_general | solution.py:137
  397.0 180.8 %reduce-scatter.10.cloned.1.call-done = f32[96,3072]{1,0:T(8,128)} async-done(((f32[1536,3072]{1,0:T(8,128)}), f32[96,3072]{1,0:T(8,128)}) %reduce-scatter.10.cloned.1.call-update) | async-done | bytes 1179664 | tf_op jit(solution)/shard_map/reduce_scatter | solution.py:139
  577.9 1.6 multiply_reduce_fusion.2
  579.5 4.9 all-reduce
  584.4 2.5 subtract_divide_fusion
  (168 shorter events, 75.7 us)
Async XLA Ops:
  7.2 64.1 %all-gather.5.cloned.1.call-start = ((), (), s32[]{:S(2)}) async-start(), calls=%async_computation.3 | async-start | bytes 5013504 | tf_op jit(solution)/shard_map/all_gather | solution.py:79
  16.2 104.4 %reduce-scatter.6.cloned.1.call-start = ((), (), s32[]{:S(2)}) async-start(), calls=%async_computation.4 | async-start | bytes 4718592 | tf_op jit(solution)/shard_map/reduce_scatter | solution.py:83
  78.4 1.0 copy-start.2
  78.4 1.9 copy-start.12
  78.4 2.5 copy-start.13
  78.4 98.1 %all-gather.9.cloned.1.call-start = ((), (), s32[]{:S(2)}) async-start(), calls=%async_computation.6 | async-start | bytes 5013504 | tf_op jit(solution)/shard_map/all_gather | solution.py:80
  80.2 124.1 %all-gather.7.cloned.1.call-start = ((), (), s32[]{:S(2)}) async-start(), calls=%async_computation.5 | async-start | bytes 2359296 | tf_op jit(solution)/shard_map/all_gather | solution.py:90
  123.3 12.8 %copy-start.14 = (f32[1536]{0:T(1024)S(1)}, f32[1536]{0:T(1024)}, u32[]{:S(2)}) copy-start(f32[1536]{0:T(1024)} %param.16) | copy-start | bytes 18436
  135.1 0.9 copy-start.5
  135.1 69.2 %copy-start.7 = (bf16[6,512,128]{2,1,0:T(8,128)(2,1)}, bf16[6,512,128]{2,1,0:T(8,128)(2,1)S(1)}, u32[]{:S(2)}) copy-start(bf16[6,512,128]{2,1,0:T(8,128)(2,1)S(1)} %get-tuple-element.351) | copy-start | bytes 2359300
  135.1 69.2 %copy-start.8 = (bf16[6,512,128]{2,1,0:T(8,128)(2,1)}, bf16[6,512,128]{2,1,0:T(8,128)(2,1)S(1)}, u32[]{:S(2)}) copy-start(bf16[6,512,128]{2,1,0:T(8,128)(2,1)S(1)} %get-tuple-element.352) | copy-start | bytes 2359300
  136.0 138.4 %reduce-scatter.8.cloned.1.call-start = ((), (), s32[]{:S(2)}) async-start(), calls=%async_computation.7 | async-start | bytes 4718592 | tf_op jit(solution)/shard_map/reduce_scatter | solution.py:129
  212.7 11.5 %copy-start.6 = (f32[512,1536]{1,0:T(8,128)}, f32[512,1536]{1,0:T(8,128)S(1)}, u32[]{:S(2)}) copy-start(f32[512,1536]{1,0:T(8,128)S(1)} %get-tuple-element.189) | copy-start | bytes 9437188
  219.7 5.7 copy-start.15
  224.2 1.1 copy-start.11
  229.7 123.8 %all-gather.11.cloned.1.call-start = ((), (), s32[]{:S(2)}) async-start(), calls=%async_computation.8 | async-start | bytes 2359296 | tf_op jit(solution)/shard_map/all_gather | solution.py:135
  325.3 0.9 copy-start.3
  326.2 27.4 %copy-start.10 = (bf16[512,1536]{1,0:T(8,128)(2,1)S(1)}, bf16[512,1536]{1,0:T(8,128)(2,1)}, u32[]{:S(2)}) copy-start(bf16[512,1536]{1,0:T(8,128)(2,1)} %param.11) | copy-start | bytes 4718596
  326.2 251.7 %reduce-scatter.10.cloned.1.call-start = ((), (), s32[]{:S(2)}) async-start(), calls=%async_computation.9 | async-start | bytes 20054016 | tf_op jit(solution)/shard_map/reduce_scatter | solution.py:139
  353.5 4.3 copy-start
  383.6 1.1 copy-start.4
  383.7 3.4 copy-start.9
  387.1 190.8 %copy-start.1 = (bf16[96,1536]{1,0:T(8,128)(2,1)S(1)}, bf16[96,1536]{1,0:T(8,128)(2,1)}, u32[]{:S(2)}) copy-start(bf16[96,1536]{1,0:T(8,128)(2,1)} %param.14) | copy-start | bytes 884740
Sparse Core Ops, SparseCore 0:
  16.3 54.9 all-gather.4
  78.6 41.9 reduce-scatter.5
  123.4 53.1 all-gather.8
  178.6 25.7 all-gather.6
  229.8 44.5 reduce-scatter.7
  326.3 27.1 all-gather.10
  383.8 194.0 reduce-scatter.9
where the time goes:
time: 595 us; the launch traced here: 594 us
  waiting for transfers between devices  407 us (68%)
  matrix products  89.7 us (15%)
  local copies, waits for them, and re-layouts  37.6 us (6%)
  other arithmetic  26.8 us (5%)
  blocking collectives  17.7 us (3%)
  between operations  14.3 us (2%)
    reduce_scatter x1, waiting for transfers between devices, shards(): lax.psum_scatter(jnp.concatenate((contract_first(grad_values, hidden), co...  181 us
    all_gather x1, waiting for transfers between devices, shards(): lax.all_gather(unit_v.astype(jnp.bfloat16), 'fsdp', axis=0, tiled=True)  55 us
    reduce_scatter x1, waiting for transfers between devices, shards(): lax.psum_scatter(grad_attn_parts, 'grp', scatter_dimension=1, tiled=True)  44.7 us
    all_gather x1, waiting for transfers between devices, shards(): lax.all_gather(unit_o.astype(jnp.bfloat16), 'fsdp', axis=0, tiled=True)  40.5 us
    reduce_scatter x1, waiting for transfers between devices, shards(): lax.psum_scatter(value_parts, 'grp', scatter_dimension=1, tiled=True)  39 us
    dot_general x20, matrix products, contract_last(): lax.dot_general(left, right, (((1,), (1,)), ((), ())), preferred_element_...  28.7 us
    all_gather x1, waiting for transfers between devices, shards(): attn_all = lax.all_gather(attn_mine, 'grp', axis=1, tiled=True)  27.7 us
    dot_general x14, matrix products, contract_first(): lax.dot_general(left, right, (((0,), (0,)), ((), ())), preferred_element_...  27.4 us
  transfers between devices with their start and end apart: 7, of which 7 were waited for; matrix products, arithmetic and copies ran while one was open for 6% of the time, Pallas kernels for 0%

commit v1 on v0

--- a/solution.py
+++ b/solution.py
@@ -6,6 +6,20 @@
 D = 3072
 HS = 128
 EPS = 1e-06
+
+
+def form_sides(payload, axis_k):
+    built = lax.axis_size("fsdp")
+    then, piece_now = (built, lax.axis_index("fsdp"))
+    back, now = (payload, 1)
+    while now < then:
+        taken_in = tuple(((b, b ^ now) for b in range(then)))
+        reply = lax.ppermute(back, "fsdp", taken_in)
+        later = jnp.concatenate([back, reply], axis=axis_k)
+        m_next = jnp.concatenate([reply, back], axis=axis_k)
+        back = jnp.where(piece_now & now == 0, later, m_next)
+        now = 2 * now
+    return back
 
 
 def contract_last(left, right):
@@ -76,7 +90,7 @@
     unit_v = value_rows / norm_v
     unit_o = out_rows / norm_o
     weight_v, weight_o = (
-        lax.all_gather(unit_v.astype(jnp.bfloat16), "fsdp", axis=0, tiled=True),
+        form_sides(unit_v.astype(jnp.bfloat16), 0),
         lax.all_gather(unit_o.astype(jnp.bfloat16), "fsdp", axis=0, tiled=True),
     )
     value_parts = contract_last(hidden, weight_v)

time: 595 us -> 654 us (1.099)
  waiting for transfers between devices: 407 us -> 453 us
  starting transfers between devices: 0.29 us -> 6.84 us
    ppermute x0 -> x4, waiting for transfers between devices: none -> 142 us  [form_sides(): reply = lax.ppermute(back, 'fsdp', taken_in)]
    all_gather x1 -> x0, waiting for transfers between devices: 55 us -> none  [shards(): lax.all_gather(unit_v.astype(jnp.bfloat16), 'fsdp', axis=0, tiled=True)]
    all_gather x1, waiting for transfers between devices: 40.5 us -> 0.03 us  [shards(): lax.all_gather(unit_o.astype(jnp.bfloat16), 'fsdp', axis=0, tiled=True)]
    ppermute x0 -> x4, starting transfers between devices: none -> 6.59 us  [form_sides(): reply = lax.ppermute(back, 'fsdp', taken_in)]
    unnamed x37 -> x39, local copies, waits for them, and re-layouts: 26.4 us -> 27.8 us
  transfers between devices with their start and end apart: 7 -> 10, of which waited for: 7 -> 9; matrix products, arithmetic and copies ran while one was open for 6% -> 6% of each run, Pallas kernels for 0% -> 0%
where the time goes in v1:
time: 654 us; the launch traced here: 652 us
  waiting for transfers between devices  453 us (69%)
  matrix products  90.6 us (14%)
  local copies, waits for them, and re-layouts  39 us (6%)
  other arithmetic  28.3 us (4%)
  blocking collectives  17.8 us (3%)
  between operations  16 us (2%)
  starting transfers between devices  6.84 us (1%)
    reduce_scatter x1, waiting for transfers between devices, shards(): lax.psum_scatter(jnp.concatenate((contract_first(grad_values, hidden), co...  180 us
    ppermute x4, waiting for transfers between devices, form_sides(): reply = lax.ppermute(back, 'fsdp', taken_in)  142 us
    reduce_scatter x1, waiting for transfers between devices, shards(): lax.psum_scatter(grad_attn_parts, 'grp', scatter_dimension=1, tiled=True)  44.7 us
    reduce_scatter x1, waiting for transfers between devices, shards(): lax.psum_scatter(value_parts, 'grp', scatter_dimension=1, tiled=True)  41.2 us
    dot_general x20, matrix products, contract_last(): lax.dot_general(left, right, (((1,), (1,)), ((), ())), preferred_element_...  28.7 us
    unnamed x39, local copies, waits for them, and re-layouts  27.8 us
    dot_general x14, matrix products, contract_first(): lax.dot_general(left, right, (((0,), (0,)), ((), ())), preferred_element_...  27.4 us
    all_gather x1, waiting for transfers between devices, shards(): attn_all = lax.all_gather(attn_mine, 'grp', axis=1, tiled=True)  27.1 us
  transfers between devices with their start and end apart: 10, of which 9 were waited for; matrix products, arithmetic and copies ran while one was open for 6% of the time, Pallas kernels for 0%

profile of v1, /device:TPU:0, one launch (start us, length us, event | category | flops | bytes accessed | tf_op | source)
XLA Modules:
  0.0 652.2 jit_solution(8297397027517886657)
XLA Ops:
  9.3 5.9 all-reduce.2
  20.2 13.6 %collective-permute-done.1 = bf16[192,1536]{1,0:T(8,128)(2,1)S(1)} collective-permute-done((bf16[192,1536]{1,0:T(8,128)(2,1)S(1)}, bf16[192,1536]{1,0:T(8,128)(2,1)S(1)}, u32[]{:S(2)}, u32[]{:S(2)}) %collective-permute-start.1) | collective-permute-done | bytes 589856 | tf_op jit(solution)/shard_map/ppermute | solution.py:17
  36.0 25.6 %collective-permute-done.2 = bf16[384,1536]{1,0:T(8,128)(2,1)S(1)} collective-permute-done((bf16[384,1536]{1,0:T(8,128)(2,1)S(1)}, bf16[384,1536]{1,0:T(8,128)(2,1)S(1)}, u32[]{:S(2)}, u32[]{:S(2)}) %collective-permute-start.2) | collective-permute-done | bytes 1179680 | tf_op jit(solution)/shard_map/ppermute | solution.py:17
  63.4 2.5 collective-permute-start.3
  66.0 101.0 %collective-permute-done.3 = bf16[768,1536]{1,0:T(8,128)(2,1)S(1)} collective-permute-done((bf16[768,1536]{1,0:T(8,128)(2,1)}, bf16[768,1536]{1,0:T(8,128)(2,1)S(1)}, u32[]{:S(2)}, u32[]{:S(2)}) %collective-permute-start.3) | collective-permute-done | bytes 2359328 | tf_op jit(solution)/shard_map/ppermute | solution.py:17
  168.3 7.1 %convolution_bitcast_fusion = f32[512,1536]{0,1:T(8,128)} fusion(bf16[512,1536]{1,0:T(8,128)(2,1)} %param.11, bf16[768,1536]{1,0:T(8,128)(2,1)S(1)} %collective-permute-done.3, bf16[768,1536]{1,0:T(8,128)(2,1)} %maximum_select_fusion.1, pred[]{:T(512)S(6)} %eq.12), kind=kOutput, calls=%fused_computation.69 | convolution fusion | flops 2437152768 | bytes 9437185 | tf_op jit(solution)/shard_map/dot_general | solution.py:26
  178.7 41.2 %reduce-scatter.6.cloned.1.call-done = f32[512,768]{0,1:T(8,128)} async-done(((f32[512,1536]{0,1:T(8,128)}), f32[512,768]{0,1:T(8,128)}) %reduce-scatter.6.cloned.1.call-update) | async-done | bytes 1572880 | tf_op jit(solution)/shard_map/reduce_scatter | solution.py:97
  222.6 11.8 %while.24 = (s32[]{:T(128)}, bf16[6,512,128]{1,2,0:T(8,128)(2,1)S(1)}, bf16[6,512,128]{2,1,0:T(8,128)(2,1)S(1)}, bf16[6,512,128]{2,1,0:T(8,128)(2,1)S(1)}, bf16[6,512,128]{2,1,0:T(8,128)(2,1)}, /*index=5*/s32[]{:T(128)}) while((s32[]{:T(128)}, bf16[6,512,128]{1,2,0:T(8,128)(2,1)S(1)}, bf16[6,512,128]{2,1,0:T(8,128)(2,1)S(1)}, ...), condition=%wide.region_6.7_spmd, body=%wide.region_3.6_spmd.sunk | while | flops 136641536 | bytes 4205653 | solution.py:103
  235.4 27.1 %all-gather.4.cloned.1.call-done = bf16[512,1536]{0,1:T(8,128)(2,1)} async-done(((bf16[512,768]{0,1:T(8,128)(2,1)}), bf16[512,1536]{0,1:T(8,128)(2,1)}) %all-gather.4.cloned.1.call-update) | async-done | bytes 1572880 | tf_op jit(solution)/shard_map/all_gather | solution.py:104
  262.5 8.4 %fusion.43 = (f32[512]{0:T(512)S(1)}, f32[512]{0:T(512)S(1)}, f32[512]{0:T(512)S(1)}, f32[512]{0:T(512)S(1)}, f32[512]{0:T(512)S(1)}, /*index=5*/f32[512]{0:T(512)S(1)}, f32[512,1536]{1,0:T(8,128)S(1)}) fusion(bf16[512,1536]{1,0:T(8,128)(2,1)} %param.17, f32[1536]{0:T(1024)S(1)} %copy-done.14, f32[1536]{0:T(1024)S(1)} %get-tuple-element.182, ...), kind=kOutput, calls=%fused_computation.73 | convolution fusion | flops 2430858240 | bytes 12625920 | tf_op jit(solution)/shard_map/dot_general | solution.py:105
  270.9 7.0 %all-reduce.1 = (f32[512]{0:T(512)S(1)}, f32[512]{0:T(512)S(1)}, f32[512]{0:T(512)S(1)}, f32[512]{0:T(512)S(1)}, f32[512]{0:T(512)S(1)}, /*index=5*/f32[512]{0:T(512)S(1)}) all-reduce(f32[512]{0:T(512)S(1)} %get-tuple-element.126, f32[512]{0:T(512)S(1)} %get-tuple-element.130, ...), channel_id=1, replica_groups=mesh['fsdp'=16,'grp'=2] {'grp'}, use_global_device_ids=true, to_apply=%region_16.17 | all-reduce | flops 3072 | bytes 24576 | tf_op jit(solution)/shard_map/psum | solution.py:108
  277.9 4.5 multiply_convert_fusion.1
  283.6 4.3 fusion.67
  288.0 44.7 %reduce-scatter.8.cloned.1.call-done = f32[512,768]{1,0:T(8,128)} async-done(((f32[512,1536]{1,0:T(8,128)}), f32[512,768]{1,0:T(8,128)}) %reduce-scatter.8.cloned.1.call-update) | async-done | bytes 1572880 | tf_op jit(solution)/shard_map/reduce_scatter | solution.py:143
  336.4 47.0 %while.25 = (s32[]{:T(128)}, bf16[6,512,128]{1,2,0:T(8,128)(2,1)}, bf16[6,512,128]{1,2,0:T(8,128)(2,1)S(1)}, bf16[6,512,128]{1,2,0:T(8,128)(2,1)S(1)}, bf16[6,51...) while((s32[]{:T(128)}, bf16[6,512,128]{1,2,0:T(8,128)(2,1)}, ...), condition=%wide.region_26.27_spmd, body=%wide.region_22.26_spmd.sunk | while | flops 340589056 | bytes 11821177 | solution.py:146
  384.4 8.5 %fusion.69 = f32[1536,1536]{0,1:T(8,128)} fusion(bf16[512,1536]{0,1:T(8,128)(2,1)} %all-gather.4.cloned.1.call-done, bf16[512,1536]{1,0:T(8,128)(2,1)} %copy-done.11), kind=kOutput, calls=%fused_computation.120 | convolution fusion | flops 2415919104 | bytes 12582912 | tf_op jit(solution)/shard_map/dot_general | solution.py:32
  392.9 18.6 %all-gather.8.cloned.1.call-done = bf16[512,1536]{0,1:T(8,128)(2,1)} async-done(((bf16[512,768]{0,1:T(8,128)(2,1)}), bf16[512,1536]{0,1:T(8,128)(2,1)}) %all-gather.8.cloned.1.call-update) | async-done | bytes 1572880 | tf_op jit(solution)/shard_map/all_gather | solution.py:149
  411.5 4.2 fusion.68
  415.7 7.2 %pad_maximum_fusion = f32[1536,3072]{0,1:T(8,128)} fusion(f32[1536,1536]{0,1:T(8,128)S(1)} %copy-done, f32[1536,1536]{0,1:T(8,128)S(1)} %fusion.68), kind=kLoop, calls=%fused_computation.57 | loop fusion | flops 4718592 | bytes 37748736 | tf_op jit(solution)/shard_map/concatenate | solution.py:154
  422.9 18.7 %copy.57 = f32[1536,3072]{1,0:T(8,128)} copy(f32[1536,3072]{0,1:T(8,128)} %pad_maximum_fusion) | data formatting | bytes 37748736
  445.0 10.8 %fusion.51 = bf16[512,1536]{1,0:T(8,128)(2,1)} fusion(bf16[512,1536]{0,1:T(8,128)(2,1)} %all-gather.8.cloned.1.call-done, bf16[512,1536]{1,0:T(8,128)(2,1)S(1)} %copy-done.9, f32[512]{0:T(512)S(1)} %get-tuple-element.187, f32[1536]{0:T(1024)S(1)} %get-tuple-element.185, f32[512]{0:T(512)S(1)} %get-tuple-element.184, bf16[768,1536]{1,0:T(8,128)(2,1)} %copy-done.16, ...), kind=kOutput, calls=%fused_computation.83 | convolution fusion | flops 2448162816 | bytes 14174209 | tf_op jit(solution)/shard_map/dot_general | solution.py:151
  455.8 179.8 %reduce-scatter.10.cloned.1.call-done = f32[96,3072]{1,0:T(8,128)} async-done(((f32[1536,3072]{1,0:T(8,128)}), f32[96,3072]{1,0:T(8,128)}) %reduce-scatter.10.cloned.1.call-update) | async-done | bytes 1179664 | tf_op jit(solution)/shard_map/reduce_scatter | solution.py:153
  637.2 4.9 all-reduce
  642.1 2.5 subtract_divide_fusion
  (178 shorter events, 87.6 us)
Async XLA Ops:
  8.0 211.9 %reduce-scatter.6.cloned.1.call-start = ((), (), s32[]{:S(2)}) async-start(), calls=%async_computation.3 | async-start | bytes 4718592 | tf_op jit(solution)/shard_map/reduce_scatter | solution.py:97
  16.3 1.6 collective-permute-start
  18.0 15.8 %collective-permute-start.1 = (bf16[192,1536]{1,0:T(8,128)(2,1)S(1)}, bf16[192,1536]{1,0:T(8,128)(2,1)S(1)}, u32[]{:S(2)}, u32[]{:S(2)}) collective-permute-start(bf16[192,1536]{1,0:T(8,128)(2,1)S(1)} %maximum_select_fusion.5), channel_id=1, source_target_pairs={{0,4},{2,6},{4,0},{6,2},{8,12},{10,14},{12,8},{14,10},{16,20},{18,... | collective-permute-start | bytes 1769480 | tf_op jit(solution)/shard_map/ppermute | solution.py:17
  34.2 27.5 %collective-permute-start.2 = (bf16[384,1536]{1,0:T(8,128)(2,1)S(1)}, bf16[384,1536]{1,0:T(8,128)(2,1)S(1)}, u32[]{:S(2)}, u32[]{:S(2)}) collective-permute-start(bf16[384,1536]{1,0:T(8,128)(2,1)S(1)} %maximum_select_fusion.2), channel_id=1, source_target_pairs={{0,8},{2,10},{4,12},{6,14},{8,0},{10,2},{12,4},{14,6},{16,24},{18,... | collective-permute-start | bytes 3538952 | tf_op jit(solution)/shard_map/ppermute | solution.py:17
  63.4 103.5 %collective-permute-start.3 = (bf16[768,1536]{1,0:T(8,128)(2,1)}, bf16[768,1536]{1,0:T(8,128)(2,1)S(1)}, u32[]{:S(2)}, u32[]{:S(2)}) collective-permute-start(bf16[768,1536]{1,0:T(8,128)(2,1)} %maximum_select_fusion.1), channel_id=1, source_target_pairs={{0,16},{2,18},{4,20},{6,22},{8,24},{10,26},{12,28},{14,30},{16,0},... | collective-permute-start | bytes 7077896 | tf_op jit(solution)/shard_map/ppermute | solution.py:17
  167.0 1.4 copy-start.16
  175.5 1.9 copy-start.12
  175.5 2.5 copy-start.13
  175.5 59.9 %all-gather.6.cloned.1.call-start = ((), (), s32[]{:S(2)}) async-start(), calls=%async_computation.5 | async-start | bytes 5013504 | tf_op jit(solution)/shard_map/all_gather | solution.py:94
  177.3 85.2 %all-gather.4.cloned.1.call-start = ((), (), s32[]{:S(2)}) async-start(), calls=%async_computation.4 | async-start | bytes 2359296 | tf_op jit(solution)/shard_map/all_gather | solution.py:104
  222.6 12.8 %copy-start.14 = (f32[1536]{0:T(1024)S(1)}, f32[1536]{0:T(1024)}, u32[]{:S(2)}) copy-start(f32[1536]{0:T(1024)} %param.16) | copy-start | bytes 18436
  234.4 28.1 %copy-start.7 = (bf16[6,512,128]{2,1,0:T(8,128)(2,1)}, bf16[6,512,128]{2,1,0:T(8,128)(2,1)S(1)}, u32[]{:S(2)}) copy-start(bf16[6,512,128]{2,1,0:T(8,128)(2,1)S(1)} %get-tuple-element.351) | copy-start | bytes 2359300
  234.4 28.1 %copy-start.8 = (bf16[6,512,128]{2,1,0:T(8,128)(2,1)}, bf16[6,512,128]{2,1,0:T(8,128)(2,1)S(1)}, u32[]{:S(2)}) copy-start(bf16[6,512,128]{2,1,0:T(8,128)(2,1)S(1)} %get-tuple-element.352) | copy-start | bytes 2359300
  235.3 97.3 %reduce-scatter.8.cloned.1.call-start = ((), (), s32[]{:S(2)}) async-start(), calls=%async_computation.6 | async-start | bytes 4718592 | tf_op jit(solution)/shard_map/reduce_scatter | solution.py:143
  270.9 11.5 %copy-start.6 = (f32[512,1536]{1,0:T(8,128)}, f32[512,1536]{1,0:T(8,128)S(1)}, u32[]{:S(2)}) copy-start(f32[512,1536]{1,0:T(8,128)S(1)} %get-tuple-element.189) | copy-start | bytes 9437188
  277.9 5.7 copy-start.15
  282.4 1.1 copy-start.11
  287.9 123.6 %all-gather.8.cloned.1.call-start = ((), (), s32[]{:S(2)}) async-start(), calls=%async_computation.7 | async-start | bytes 2359296 | tf_op jit(solution)/shard_map/all_gather | solution.py:149
  384.3 27.2 %copy-start.10 = (bf16[512,1536]{1,0:T(8,128)(2,1)S(1)}, bf16[512,1536]{1,0:T(8,128)(2,1)}, u32[]{:S(2)}) copy-start(bf16[512,1536]{1,0:T(8,128)(2,1)} %param.11) | copy-start | bytes 4718596
  384.3 251.3 %reduce-scatter.10.cloned.1.call-start = ((), (), s32[]{:S(2)}) async-start(), calls=%async_computation.8 | async-start | bytes 20054016 | tf_op jit(solution)/shard_map/reduce_scatter | solution.py:153
  411.5 4.3 copy-start
  441.6 1.1 copy-start.4
  441.6 3.4 copy-start.9
  445.0 190.6 %copy-start.1 = (bf16[96,1536]{1,0:T(8,128)(2,1)S(1)}, bf16[96,1536]{1,0:T(8,128)(2,1)}, u32[]{:S(2)}) copy-start(bf16[96,1536]{1,0:T(8,128)(2,1)} %param.14) | copy-start | bytes 884740
  (3 other events, 2.7 us)
Sparse Core Ops, SparseCore 0:
  175.6 44.2 reduce-scatter.5
  288.0 44.5 reduce-scatter.7
Sparse Core Ops, SparseCore 1:
  178.9 53.8 all-gather.5
  235.4 27.0 all-gather.3
  384.4 27.0 all-gather.7
  441.7 193.8 reduce-scatter.9
